TPU v7x, 32 devices: a whole 2x2x4 slice. The times are simulated.
32 devices in a mesh: heads: 4 (over y, core), blk: 8 (over z, x).
Axes of the slice: x: 2, y: 2, z: 4, core: 2. Of those that a mesh axis runs over, the one named last changes fastest.
Arguments:
- tokens: bfloat16 [4096, 4096], P(('blk', 'heads')), may hold values from -6 to 6
- w_query: bfloat16 [4096, 2048], P('blk', 'heads'), may hold values from -0.75 to 0.75
- key_value_weight: bfloat16 [4096, 2, 512], P('blk', None, 'heads'), may hold values from -0.75 to 0.75
- w_out: bfloat16 [2048, 4096], P(('heads', 'blk')), may hold values from -0.5 to 0.5
- doc_lengths: int32 [16], replicated, may hold values from 1 to 1024, 4096 in all
Outputs:
- attended: bfloat16 [4096, 4096], P(('blk', 'heads'))
Inputs may be any that keep to these rules, and one draw needn't show every extreme that they name: `doc_lengths`: the 16 lengths sum to 4096; the longest document has exactly 1024 tokens.
All inputs are finite; a program needn't handle non-finite values.
Results may differ from a plain program's by a relative error of at most 0.012.
Values may be sent and summed in bfloat16 or wider, within the bound.
A program may use at most 128 MiB of HBM per device.

v0:
```python
import jax
import jax.numpy as jnp
from jax import lax
from jax.sharding import PartitionSpec as P

HEAD_SIZE = 128
norm_epsilon = 1e-05
rope_base = 500000.0
masked_score = -1e30


def shifted(value, axis, steps):
    count = lax.axis_size(axis)
    first, last = (max(0, -steps), min(count, count - steps))
    return lax.ppermute(value, axis, [(source, source + steps) for source in range(first, last)])


def locate_documents(positions, doc_lengths):
    ends = jnp.cumsum(doc_lengths)
    after = positions[:, None] >= ends[None, :]
    ident = jnp.sum(after.astype(jnp.int32), axis=1)
    starts = jnp.sum(jnp.where(after, doc_lengths[None, :], 0), axis=1)
    return (ident, starts)


def apply_rotation(values, relative_offset):
    half = values.shape[-1] // 2
    freqs = jnp.power(rope_base, -2.0 * jnp.arange(half, dtype=jnp.float32) / values.shape[-1])
    angle = relative_offset.astype(jnp.float32)[:, None] * freqs[None, :]
    cosine = jnp.cos(angle)[:, None, :]
    sine = jnp.sin(angle)[:, None, :]
    first = values[..., :half]
    second = values[..., half:]
    return jnp.concatenate(
        [first * cosine - second * sine, second * cosine + first * sine], axis=-1
    )


def on_device(tokens, w_query, key_value_weight, w_out, doc_lengths):
    blk_index = lax.axis_index("blk")
    reach = lax.axis_size("blk") // 4
    values = tokens.astype(jnp.float32)
    normalized_input = (
        values * lax.rsqrt(jnp.mean(values * values, axis=1, keepdims=True) + norm_epsilon)
    ).astype(jnp.bfloat16)
    block_input = lax.all_gather(normalized_input, "heads", axis=0, tiled=True)
    block_rows = block_input.shape[0]
    query_cols = w_query.shape[1]
    kv_cols = key_value_weight.shape[2]
    pieces = (
        lax.all_gather(w_query, "blk", axis=0, tiled=True),
        lax.all_gather(key_value_weight, "blk", axis=0, tiled=True),
    )
    count = pieces[0].shape[0]
    query_part = jnp.dot(block_input, pieces[0], preferred_element_type=jnp.float32)
    keyval_part = jnp.dot(
        block_input, pieces[1].reshape(count, 2 * kv_cols), preferred_element_type=jnp.float32
    )
    positions = blk_index * block_rows + jnp.arange(block_rows, dtype=jnp.int32)
    ident, starts = locate_documents(positions, doc_lengths)
    relative_offset = positions - starts
    query_heads = query_cols // HEAD_SIZE
    kv_heads = kv_cols // HEAD_SIZE
    head_group = query_heads // kv_heads
    query_rows = apply_rotation(
        query_part.reshape(block_rows, query_heads, HEAD_SIZE), relative_offset
    ).astype(jnp.bfloat16)
    query_rows = query_rows.reshape(block_rows, kv_heads, head_group, HEAD_SIZE)
    rotated_keys = apply_rotation(
        keyval_part[:, :kv_cols].reshape(block_rows, kv_heads, HEAD_SIZE), relative_offset
    ).astype(jnp.bfloat16)
    value_rows = (
        keyval_part[:, kv_cols:].reshape(block_rows, kv_heads, HEAD_SIZE).astype(jnp.bfloat16)
    )
    kv_block = jnp.stack([rotated_keys, value_rows], axis=1)
    scale = HEAD_SIZE ** (-0.5)

    def attend_tile(state, kv_now, distance):
        key_pos = (blk_index - distance) * block_rows + jnp.arange(block_rows, dtype=jnp.int32)
        key_doc, unused_k = locate_documents(key_pos, doc_lengths)
        keep = (
            (key_pos[None, :] >= 0)
            & (key_pos[None, :] <= positions[:, None])
            & (key_doc[None, :] == ident[:, None])
        )
        highest, totals, accum = state
        scores = (
            jnp.einsum(
                "qhgd,khd->hgqk", query_rows, kv_now[:, 0], preferred_element_type=jnp.float32
            )
            * scale
        )
        scores = jnp.where(keep, scores, masked_score)
        new_high = jnp.maximum(highest, jnp.max(scores, axis=-1))
        fading = jnp.exp(highest - new_high)
        probs = jnp.where(keep, jnp.exp(scores - new_high[..., None]), 0.0)
        totals = totals * fading + jnp.sum(probs, axis=-1)
        update = jnp.einsum(
            "hgqk,khd->hgqd",
            probs.astype(jnp.bfloat16),
            kv_now[:, 1],
            preferred_element_type=jnp.float32,
        )
        accum = accum * fading[..., None] + update
        return (new_high, totals, accum)

    initial = (
        jnp.full((kv_heads, head_group, block_rows), masked_score, jnp.float32),
        jnp.zeros((kv_heads, head_group, block_rows), jnp.float32),
        jnp.zeros((kv_heads, head_group, block_rows, HEAD_SIZE), jnp.float32),
    )
    state = attend_tile(initial, kv_block, 0)

    def advance(distance, carry):
        kv_now, inner = carry
        kv_now = shifted(kv_now, "blk", 1)
        return (kv_now, attend_tile(inner, kv_now, distance))

    unused_kv, state = lax.fori_loop(1, reach + 1, advance, (kv_block, state))
    highest, totals, accum = state
    mixed = accum / totals[..., None]
    mixed = mixed.transpose(2, 0, 1, 3).reshape(block_rows, query_cols).astype(jnp.bfloat16)
    head_rows = lax.all_gather(w_out, "blk", axis=0, tiled=True)
    return lax.psum_scatter(
        jnp.dot(mixed, head_rows, preferred_element_type=jnp.float32).astype(jnp.bfloat16),
        "heads",
        scatter_dimension=0,
        tiled=True,
    )


def solution(mesh):
    return jax.shard_map(
        on_device,
        mesh=mesh,
        in_specs=(
            P(("blk", "heads"), None),
            P("blk", "heads"),
            P("blk", None, "heads"),
            P(("heads", "blk"), None),
            P(),
        ),
        out_specs=P(("blk", "heads"), None),
        check_vma=False,
    )
```

profile of v0, /device:TPU:0, one launch (start us, length us, event | category | flops | bytes accessed | tf_op | source)
XLA Modules:
  0.0 311.8 jit_solution(1493680241664175790)
XLA Ops:
  6.5 0.7 all-gather.7.cloned.1.call-update
  7.3 0.0 all-gather.5.cloned.1.call-start
  7.3 1.5 fusion.24
  8.8 2.5 fusion.25
  11.3 0.0 all-gather.9.cloned.1.call-start
  11.4 0.7 all-gather.9.cloned.1.call-update
  12.1 0.5 all-gather.11.cloned.1.call-update
  12.6 0.0 reduce-scatter.2.cloned.1.call-start
  12.7 0.2 broadcast_in_dim.114
  12.9 0.1 fusion.56
  13.0 1.0 multiply_cosine_fusion
  14.0 0.4 compare_and_fusion.1
  14.4 46.9 %all-gather.7.cloned.1.call-done = bf16[4096,2,128]{2,1,0:T(2,128)(2,1)} async-done(((bf16[512,2,128]{2,1,0:T(2,128)(2,1)}), bf16[4096,2,128]{2,1,0:T(2,128)(2,1)}) %all-gather.7.cloned.1.call-update) | async-done | bytes 2097168 | tf_op jit(solution)/shard_map/all_gather | solution.py:52
  61.3 34.6 %all-gather.5.cloned.1.call-done = bf16[512,4096]{1,0:T(8,128)(2,1)} async-done(((bf16[128,4096]{1,0:T(8,128)(2,1)}), bf16[512,4096]{1,0:T(8,128)(2,1)}) %all-gather.5.cloned.1.call-update) | async-done | bytes 4194320 | tf_op jit(solution)/shard_map/all_gather | solution.py:46
  95.9 4.2 %fusion.27 = f32[512,256]{0,1:T(8,128)S(1)} fusion(bf16[512,4096]{1,0:T(8,128)(2,1)} %all-gather.5.cloned.1.call-done, bf16[512,8,2,128]{3,2,1,0:T(2,128)(2,1)} %bitcast.161), kind=kOutput, calls=%fused_computation.38 | convolution fusion | flops 1073741824 | bytes 6815744 | tf_op jit(solution)/shard_map/dot_general | solution.py:56
  100.1 0.6 fusion.48
  100.7 0.2 copy-done
  100.9 0.8 copy.35
  101.7 69.1 %all-gather.9.cloned.1.call-done = bf16[4096,512]{1,0:T(8,128)(2,1)} async-done(((bf16[512,512]{1,0:T(8,128)(2,1)}), bf16[4096,512]{1,0:T(8,128)(2,1)}) %all-gather.9.cloned.1.call-update) | async-done | bytes 4194320 | tf_op jit(solution)/shard_map/all_gather | solution.py:51
  170.8 5.8 %fusion.64 = f32[512,512]{0,1:T(8,128)S(1)} fusion(bf16[512,4096]{1,0:T(8,128)(2,1)} %all-gather.5.cloned.1.call-done, bf16[4096,512]{1,0:T(8,128)(2,1)} %all-gather.9.cloned.1.call-done), kind=kOutput, calls=%fused_computation.92 | convolution fusion | flops 2147483648 | bytes 9437184 | tf_op jit(solution)/shard_map/dot_general | solution.py:55
  176.7 0.1 fusion.63
  176.8 0.3 copy.43
  177.1 0.3 copy.44
  177.5 0.3 subtract_convert_fusion
  177.8 0.3 pad_maximum_fusion
  178.1 1.2 fusion.21
  179.3 1.0 fusion.23
  180.4 1.6 fusion.36
  182.0 29.8 %while.22 = (s32[]{:T(128)}, bf16[512,2,1,128]{3,0,2,1:T(8,128)(2,1)S(1)}, f32[1,4,512]{2,1,0:T(4,128)S(1)}, f32[1,4,512]{2,1,0:T(4,128)S(1)}, f32[1,4,512,128]{...) while((s32[]{:T(128)}, ...), condition=%wide.region_10.11_spmd.clone, body=%wide.region_6.10_spmd.clone.sunk | while | flops 552107520 | bytes 18236672 | solution.py:119
  182.2 2.5 collective-permute-start
  184.7 0.1 convert_reduce_fusion.2
  184.8 0.3 compare_and_fusion.3
  185.1 6.1 %collective-permute-done = bf16[512,2,1,128]{3,0,2,1:T(8,128)(2,1)S(1)} collective-permute-done((bf16[512,2,1,128]{3,0,2,1:T(8,128)(2,1)S(1)}, bf16[512,2,1,128]{3,0,2,1:T(8,128)(2,1)S(1)}, u32[]{:S(2)}, u32[]{:S(2)}) %collective-permute-start) | collective-permute-done | bytes 262176 | tf_op jit(solution)/shard_map/while/body/eval_jaxpr/ppermute | solution.py:15
  191.2 0.9 fusion.76
  192.1 1.0 fusion.78
  193.2 1.9 fusion.79
  195.2 8.8 %collective-permute-start = (bf16[512,2,1,128]{3,0,2,1:T(8,128)(2,1)S(1)}, bf16[512,2,1,128]{3,0,2,1:T(8,128)(2,1)S(1)}, u32[]{:S(2)}, u32[]{:S(2)}) collective-permute-start(bf16[512,2,1,128]{3,0,2,1:T(8,128)(2,1)S(1)} %get-tuple-element.431), channel_id=1, source_target_pairs={{0,1},{1,2},{2,3},{3,4},{4,5},{5,6},{6,7},{8,9},{9,10},{10,11},{11... | collective-permute-start | bytes 786440 | tf_op jit(solution)/shard_map/while/body/eval_jaxpr/ppermute | solution.py:15
  204.0 0.1 convert_reduce_fusion.2
  204.1 0.3 compare_and_fusion.3
  204.4 3.4 %collective-permute-done = bf16[512,2,1,128]{3,0,2,1:T(8,128)(2,1)S(1)} collective-permute-done((bf16[512,2,1,128]{3,0,2,1:T(8,128)(2,1)S(1)}, bf16[512,2,1,128]{3,0,2,1:T(8,128)(2,1)S(1)}, u32[]{:S(2)}, u32[]{:S(2)}) %collective-permute-start) | collective-permute-done | bytes 262176 | tf_op jit(solution)/shard_map/while/body/eval_jaxpr/ppermute | solution.py:15
  207.8 0.9 fusion.76
  208.7 1.0 fusion.78
  209.8 1.9 fusion.79
  211.7 0.3 copy.36
  212.1 0.1 divide_convert_fusion
  212.2 41.3 %all-gather.11.cloned.1.call-done = bf16[512,4096]{1,0:T(8,128)(2,1)} async-done(((bf16[64,4096]{1,0:T(8,128)(2,1)}), bf16[512,4096]{1,0:T(8,128)(2,1)}) %all-gather.11.cloned.1.call-update) | async-done | bytes 4194320 | tf_op jit(solution)/shard_map/all_gather | solution.py:123
  253.6 6.5 %convolution_convert_fusion = bf16[512,4096]{1,0:T(8,128)(2,1)} fusion(bf16[512,512]{0,1:T(8,128)(2,1)S(1)} %bitcast.151, bf16[512,4096]{1,0:T(8,128)(2,1)} %all-gather.11.cloned.1.call-done), kind=kOutput, calls=%fused_computation.27 | convolution fusion | flops 2149580800 | bytes 8912896 | tf_op jit(solution)/shard_map/dot_general | solution.py:125
  260.1 45.2 %reduce-scatter.2.cloned.1.call-done = bf16[128,4096]{1,0:T(8,128)(2,1)} async-done(((bf16[512,4096]{1,0:T(8,128)(2,1)}), bf16[128,4096]{1,0:T(8,128)(2,1)}) %reduce-scatter.2.cloned.1.call-update) | async-done | bytes 1048592 | tf_op jit(solution)/shard_map/reduce_scatter | solution.py:124
  (33 shorter events, 0.3 us)
Async XLA Ops:
  6.5 6.2 %copy-start.3 = (s32[16]{0:T(128)S(1)}, s32[16]{0:T(128)}, u32[]{:S(2)}) copy-start(s32[16]{0:T(128)} %param.11) | copy-start | bytes 196
  6.5 54.8 %all-gather.7.cloned.1.call-start = ((), (), s32[]{:S(2)}) async-start(), calls=%async_computation.2 | async-start | bytes 2359296 | tf_op jit(solution)/shard_map/all_gather | solution.py:52
  7.3 88.6 %all-gather.5.cloned.1.call-start = ((), (), s32[]{:S(2)}) async-start(), calls=%async_computation.1 | async-start | bytes 5242880 | tf_op jit(solution)/shard_map/all_gather | solution.py:46
  11.3 159.5 %all-gather.9.cloned.1.call-start = ((), (), s32[]{:S(2)}) async-start(), calls=%async_computation.3 | async-start | bytes 4718592 | tf_op jit(solution)/shard_map/all_gather | solution.py:51
  12.1 241.5 %all-gather.11.cloned.1.call-start = ((), (), s32[]{:S(2)}) async-start(), calls=%async_computation.4 | async-start | bytes 4718592 | tf_op jit(solution)/shard_map/all_gather | solution.py:123
  12.6 292.7 %reduce-scatter.2.cloned.1.call-start = ((), (), s32[]{:S(2)}) async-start(), calls=%async_computation.5 | async-start | bytes 5242880 | tf_op jit(solution)/shard_map/reduce_scatter | solution.py:124
  100.0 0.8 copy-start
  178.1 2.3 copy-start.1
  180.4 1.6 copy-start.2
  182.2 9.1 %collective-permute-start = (bf16[512,2,1,128]{3,0,2,1:T(8,128)(2,1)S(1)}, bf16[512,2,1,128]{3,0,2,1:T(8,128)(2,1)S(1)}, u32[]{:S(2)}, u32[]{:S(2)}) collective-permute-start(bf16[512,2,1,128]{3,0,2,1:T(8,128)(2,1)S(1)} %get-tuple-element.431), channel_id=1, source_target_pairs={{0,1},{1,2},{2,3},{3,4},{4,5},{5,6},{6,7},{8,9},{9,10},{10,11},{11... | collective-permute-start | bytes 786440 | tf_op jit(solution)/shard_map/while/body/eval_jaxpr/ppermute | solution.py:15
  195.2 12.7 %collective-permute-start = (bf16[512,2,1,128]{3,0,2,1:T(8,128)(2,1)S(1)}, bf16[512,2,1,128]{3,0,2,1:T(8,128)(2,1)S(1)}, u32[]{:S(2)}, u32[]{:S(2)}) collective-permute-start(bf16[512,2,1,128]{3,0,2,1:T(8,128)(2,1)S(1)} %get-tuple-element.431), channel_id=1, source_target_pairs={{0,1},{1,2},{2,3},{3,4},{4,5},{5,6},{6,7},{8,9},{9,10},{10,11},{11... | collective-permute-start | bytes 786440 | tf_op jit(solution)/shard_map/while/body/eval_jaxpr/ppermute | solution.py:15
Sparse Core Ops, SparseCore 0:
  9.5 51.7 all-gather.6
  62.9 32.9 all-gather.4
  98.0 72.7 all-gather.8
  172.8 80.7 all-gather.10
  260.2 45.0 reduce-scatter.1
where the time goes:
time: 312 us
  waiting for transfers between devices  249 us (80%)
  matrix products  24.9 us (8%)
  between operations  13.3 us (4%)
  starting transfers between devices  11.4 us (4%)
  other arithmetic  11 us (4%)
    all_gather x1, waiting for transfers between devices, on_device(): lax.all_gather(w_query, 'blk', axis=0, tiled=True)  69.1 us
    all_gather x1, waiting for transfers between devices, on_device(): lax.all_gather(key_value_weight, 'blk', axis=0, tiled=True)  46.9 us
    reduce_scatter x1, waiting for transfers between devices, on_device(): lax.psum_scatter(jnp.dot(mixed, head_rows, preferred_element_type=jnp.flo...  45.2 us
    all_gather x1, waiting for transfers between devices, on_device(): head_rows = lax.all_gather(w_out, 'blk', axis=0, tiled=True)  41.3 us
    all_gather x1, waiting for transfers between devices, on_device(): block_input = lax.all_gather(normalized_input, 'heads', axis=0, tiled=True)  34.6 us
    ppermute x2, starting transfers between devices, shifted(): lax.ppermute(value, axis, [(source, source + steps) for source in range(f...  11.3 us
    ppermute x2, waiting for transfers between devices, shifted(): lax.ppermute(value, axis, [(source, source + steps) for source in range(f...  9.5 us
    dot_general x1, matrix products, on_device(): jnp.dot(mixed, head_rows, preferred_element_type=jnp.float32)  6.52 us
  transfers between devices with their start and end apart: 7, of which 7 were waited for; matrix products, arithmetic and copies ran while one was open for 10% of the time, Pallas kernels for 0%

commit v1 on v0

--- a/solution.py
+++ b/solution.py
@@ -43,7 +43,14 @@
     normalized_input = (
         values * lax.rsqrt(jnp.mean(values * values, axis=1, keepdims=True) + norm_epsilon)
     ).astype(jnp.bfloat16)
-    block_input = lax.all_gather(normalized_input, "heads", axis=0, tiled=True)
+    ring = [normalized_input]
+    for hop in range(3):
+        ring.append(lax.ppermute(ring[-1], "heads", [(dev, (dev + 1) % 4) for dev in range(4)]))
+    block_input = jnp.roll(
+        jnp.concatenate(ring[::-1], axis=0),
+        (lax.axis_index("heads") + 1) * ring[0].shape[0],
+        axis=0,
+    )
     block_rows = block_input.shape[0]
     query_cols = w_query.shape[1]
     kv_cols = key_value_weight.shape[2]

time: 312 us -> 277 us (0.89)
  waiting for transfers between devices: 249 us -> 200 us
  local copies, waits for them, and re-layouts: 2.21 us -> 10.9 us
  other arithmetic: 11 us -> 14.4 us
    all_gather x1, waiting for transfers between devices: 46.9 us -> 0.01 us  [on_device(): lax.all_gather(key_value_weight, 'blk', axis=0, tiled=True)]
    ppermute x0 -> x3, waiting for transfers between devices: none -> 40.4 us  [on_device(): lax.ppermute(ring[-1], 'heads', [(dev, (dev + 1) % 4) for dev in range(4)])]
    all_gather x1 -> x0, waiting for transfers between devices: 34.6 us -> none  [on_device(): block_input = lax.all_gather(normalized_input, 'heads', axis=0, tiled=True)]
    unnamed x11 -> x19, local copies, waits for them, and re-layouts: 1.69 us -> 10.4 us
    all_gather x1, waiting for transfers between devices: 69.1 us -> 63.1 us  [on_device(): lax.all_gather(w_query, 'blk', axis=0, tiled=True)]
  transfers between devices with their start and end apart: 7 -> 9, of which waited for: 7 -> 8; matrix products, arithmetic and copies ran while one was open for 10% -> 16% of each run, Pallas kernels for 0% -> 0%
where the time goes in v1:
time: 277 us
  waiting for transfers between devices  200 us (72%)
  matrix products  24.8 us (9%)
  other arithmetic  14.4 us (5%)
  between operations  13.4 us (5%)
  starting transfers between devices  12.8 us (5%)
  local copies, waits for them, and re-layouts  10.9 us (4%)
    all_gather x1, waiting for transfers between devices, on_device(): lax.all_gather(w_query, 'blk', axis=0, tiled=True)  63.1 us
    reduce_scatter x1, waiting for transfers between devices, on_device(): lax.psum_scatter(jnp.dot(mixed, head_rows, preferred_element_type=jnp.flo...  44.3 us
    all_gather x1, waiting for transfers between devices, on_device(): head_rows = lax.all_gather(w_out, 'blk', axis=0, tiled=True)  42.1 us
    ppermute x3, waiting for transfers between devices, on_device(): lax.ppermute(ring[-1], 'heads', [(dev, (dev + 1) % 4) for dev in range(4)])  40.4 us
    ppermute x2, starting transfers between devices, shifted(): lax.ppermute(value, axis, [(source, source + steps) for source in range(f...  12.1 us
    unnamed x19, local copies, waits for them, and re-layouts  10.4 us
    ppermute x2, waiting for transfers between devices, shifted(): lax.ppermute(value, axis, [(source, source + steps) for source in range(f...  8.61 us
    dot_general x1, matrix products, on_device(): jnp.dot(mixed, head_rows, preferred_element_type=jnp.float32)  6.49 us
  transfers between devices with their start and end apart: 9, of which 8 were waited for; matrix products, arithmetic and copies ran while one was open for 16% of the time, Pallas kernels for 0%

profile of v1, /device:TPU:0, one launch (start us, length us, event | category | flops | bytes accessed | tf_op | source)
XLA Modules:
  0.0 276.7 jit_solution(2260600273008845189)
XLA Ops:
  6.5 0.7 all-gather.4.cloned.1.call-update
  7.3 0.7 all-gather.6.cloned.1.call-update
  8.1 1.5 fusion.28
  9.6 1.5 fusion.29
  11.1 0.5 collective-permute-start.1
  11.6 14.4 %collective-permute-done.1 = bf16[128,4096]{1,0:T(8,128)(2,1)S(1)} collective-permute-done((bf16[128,4096]{1,0:T(8,128)(2,1)S(1)}, bf16[128,4096]{1,0:T(8,128)(2,1)S(1)}, u32[]{:S(2)}, u32[]{:S(2)}) %collective-permute-start.1) | collective-permute-done | bytes 1048608 | tf_op jit(solution)/shard_map/ppermute | solution.py:48
  26.1 14.1 %collective-permute-done.2 = bf16[128,4096]{1,0:T(8,128)(2,1)S(1)} collective-permute-done((bf16[128,4096]{1,0:T(8,128)(2,1)S(1)}, bf16[128,4096]{1,0:T(8,128)(2,1)S(1)}, u32[]{:S(2)}, u32[]{:S(2)}) %collective-permute-start.2) | collective-permute-done | bytes 1048608 | tf_op jit(solution)/shard_map/ppermute | solution.py:48
  40.3 0.2 broadcast_in_dim.114
  40.6 0.3 compare_and_fusion.1
  41.0 1.8 multiply_cosine_fusion
  42.8 11.8 %collective-permute-done.3 = bf16[128,4096]{1,0:T(8,128)(2,1)} collective-permute-done((bf16[128,4096]{1,0:T(8,128)(2,1)S(1)}, bf16[128,4096]{1,0:T(8,128)(2,1)}, u32[]{:S(2)}, u32[]{:S(2)}) %collective-permute-start.3) | collective-permute-done | bytes 1048608 | tf_op jit(solution)/shard_map/ppermute | solution.py:48
  54.6 2.3 constant_dynamic-update-slice_fusion.7
  56.9 1.1 constant_dynamic-update-slice_fusion.6
  58.0 1.1 constant_dynamic-update-slice_fusion.5
  59.1 1.2 constant_dynamic-update-slice_fusion.4
  60.3 2.3 constant_dynamic-update-slice_fusion.3
  62.6 1.1 constant_dynamic-update-slice_fusion.2
  63.7 1.1 constant_dynamic-update-slice_fusion.1
  64.7 1.2 constant_dynamic-update-slice_fusion
  66.0 4.2 %fusion.24 = f32[512,256]{0,1:T(8,128)S(1)} fusion(bf16[1024,4096]{1,0:T(8,128)(2,1)} %constant_dynamic-update-slice_fusion, s32[]{:T(128)S(6)} %select_n.43, bf16[512,8,2,128]{3,2,1,0:T(2,128)(2,1)} %bitcast.159), kind=kOutput, calls=%fused_computation.33 | convolution fusion | flops 1073741824 | bytes 6815748 | tf_op jit(solution)/shard_map/dot_general | solution.py:63
  70.2 0.6 fusion.51
  70.8 0.8 copy.35
  71.7 63.1 %all-gather.6.cloned.1.call-done = bf16[4096,512]{1,0:T(8,128)(2,1)} async-done(((bf16[512,512]{1,0:T(8,128)(2,1)}), bf16[4096,512]{1,0:T(8,128)(2,1)}) %all-gather.6.cloned.1.call-update) | async-done | bytes 4194320 | tf_op jit(solution)/shard_map/all_gather | solution.py:58
  134.8 5.8 %fusion.22 = f32[512,512]{0,1:T(8,128)S(1)} fusion(bf16[4096,512]{1,0:T(8,128)(2,1)} %all-gather.6.cloned.1.call-done, bf16[1024,4096]{1,0:T(8,128)(2,1)} %constant_dynamic-update-slice_fusion, s32[]{:T(128)S(6)} %select_n.43), kind=kOutput, calls=%fused_computation.31 | convolution fusion | flops 2147483648 | bytes 9437188 | tf_op jit(solution)/shard_map/dot_general | solution.py:62
  140.7 0.3 copy.44
  141.1 0.3 copy.43
  141.4 1.3 subtract_convert_fusion
  142.8 0.3 pad_maximum_fusion
  143.1 1.2 fusion.21
  144.3 1.1 fusion.27
  145.4 1.6 fusion.39
  147.0 29.7 %while.22 = (s32[]{:T(128)}, bf16[512,2,1,128]{3,0,2,1:T(8,128)(2,1)S(1)}, f32[1,4,512]{2,1,0:T(4,128)S(1)}, f32[1,4,512]{2,1,0:T(4,128)S(1)}, f32[1,4,512,128]{...) while((s32[]{:T(128)}, ...), condition=%wide.region_10.11_spmd.clone, body=%wide.region_6.10_spmd.clone.sunk | while | flops 552107520 | bytes 18236672 | solution.py:126
  147.2 2.5 collective-permute-start
  149.8 0.3 compare_and_fusion.3
  150.1 5.2 %collective-permute-done = bf16[512,2,1,128]{3,0,2,1:T(8,128)(2,1)S(1)} collective-permute-done((bf16[512,2,1,128]{3,0,2,1:T(8,128)(2,1)S(1)}, bf16[512,2,1,128]{3,0,2,1:T(8,128)(2,1)S(1)}, u32[]{:S(2)}, u32[]{:S(2)}) %collective-permute-start) | collective-permute-done | bytes 262176 | tf_op jit(solution)/shard_map/while/body/eval_jaxpr/ppermute | solution.py:15
  155.3 0.9 fusion.78
  156.2 1.0 fusion.80
  157.3 1.9 fusion.81
  159.3 9.7 %collective-permute-start = (bf16[512,2,1,128]{3,0,2,1:T(8,128)(2,1)S(1)}, bf16[512,2,1,128]{3,0,2,1:T(8,128)(2,1)S(1)}, u32[]{:S(2)}, u32[]{:S(2)}) collective-permute-start(bf16[512,2,1,128]{3,0,2,1:T(8,128)(2,1)S(1)} %get-tuple-element.431), channel_id=1, source_target_pairs={{0,1},{1,2},{2,3},{3,4},{4,5},{5,6},{6,7},{8,9},{9,10},{10,11},{11... | collective-permute-start | bytes 786440 | tf_op jit(solution)/shard_map/while/body/eval_jaxpr/ppermute | solution.py:15
  169.1 0.3 compare_and_fusion.3
  169.4 3.4 %collective-permute-done = bf16[512,2,1,128]{3,0,2,1:T(8,128)(2,1)S(1)} collective-permute-done((bf16[512,2,1,128]{3,0,2,1:T(8,128)(2,1)S(1)}, bf16[512,2,1,128]{3,0,2,1:T(8,128)(2,1)S(1)}, u32[]{:S(2)}, u32[]{:S(2)}) %collective-permute-start) | collective-permute-done | bytes 262176 | tf_op jit(solution)/shard_map/while/body/eval_jaxpr/ppermute | solution.py:15
  172.8 0.9 fusion.78
  173.7 1.0 fusion.80
  174.8 1.9 fusion.81
  176.7 0.3 copy.36
  177.2 42.1 %all-gather.8.cloned.1.call-done = bf16[512,4096]{1,0:T(8,128)(2,1)} async-done(((bf16[64,4096]{1,0:T(8,128)(2,1)}), bf16[512,4096]{1,0:T(8,128)(2,1)}) %all-gather.8.cloned.1.call-update) | async-done | bytes 4194320 | tf_op jit(solution)/shard_map/all_gather | solution.py:130
  219.4 6.5 %convolution_convert_fusion = bf16[512,4096]{1,0:T(8,128)(2,1)} fusion(bf16[512,512]{0,1:T(8,128)(2,1)S(1)} %bitcast.149, bf16[512,4096]{1,0:T(8,128)(2,1)} %all-gather.8.cloned.1.call-done), kind=kOutput, calls=%fused_computation.27 | convolution fusion | flops 2149580800 | bytes 8912896 | tf_op jit(solution)/shard_map/dot_general | solution.py:132
  225.9 44.3 %reduce-scatter.2.cloned.1.call-done = bf16[128,4096]{1,0:T(8,128)(2,1)} async-done(((bf16[512,4096]{1,0:T(8,128)(2,1)}), bf16[128,4096]{1,0:T(8,128)(2,1)}) %reduce-scatter.2.cloned.1.call-update) | async-done | bytes 1048592 | tf_op jit(solution)/shard_map/reduce_scatter | solution.py:131
  (46 shorter events, 0.9 us)
Async XLA Ops:
  6.5 33.8 %copy-start.4 = (s32[16]{0:T(128)S(1)}, s32[16]{0:T(128)}, u32[]{:S(2)}) copy-start(s32[16]{0:T(128)} %param.11) | copy-start | bytes 196
  6.5 59.5 %all-gather.4.cloned.1.call-start = ((), (), s32[]{:S(2)}) async-start(), calls=%async_computation.1 | async-start | bytes 2359296 | tf_op jit(solution)/shard_map/all_gather | solution.py:59
  7.3 127.5 %all-gather.6.cloned.1.call-start = ((), (), s32[]{:S(2)}) async-start(), calls=%async_computation.2 | async-start | bytes 4718592 | tf_op jit(solution)/shard_map/all_gather | solution.py:58
  8.0 211.4 %all-gather.8.cloned.1.call-start = ((), (), s32[]{:S(2)}) async-start(), calls=%async_computation.3 | async-start | bytes 4718592 | tf_op jit(solution)/shard_map/all_gather | solution.py:130
  11.1 48.0 %copy-start = (bf16[128,4096]{1,0:T(8,128)(2,1)S(1)}, bf16[128,4096]{1,0:T(8,128)(2,1)}, u32[]{:S(2)}) copy-start(bf16[128,4096]{1,0:T(8,128)(2,1)} %param.7) | copy-start | bytes 3145732
  11.1 15.0 %collective-permute-start.1 = (bf16[128,4096]{1,0:T(8,128)(2,1)S(1)}, bf16[128,4096]{1,0:T(8,128)(2,1)S(1)}, u32[]{:S(2)}, u32[]{:S(2)}) collective-permute-start(bf16[128,4096]{1,0:T(8,128)(2,1)S(1)} %fusion.29), channel_id=1, source_target_pairs={{0,8},{8,16},{16,24},{24,0},{1,9},{9,17},{17,25},{25,1},{2,10},{10... | collective-permute-start | bytes 3145736 | tf_op jit(solution)/shard_map/ppermute | solution.py:48
  26.1 14.2 %collective-permute-start.2 = (bf16[128,4096]{1,0:T(8,128)(2,1)S(1)}, bf16[128,4096]{1,0:T(8,128)(2,1)S(1)}, u32[]{:S(2)}, u32[]{:S(2)}) collective-permute-start(bf16[128,4096]{1,0:T(8,128)(2,1)S(1)} %collective-permute-done.1), channel_id=1, source_target_pairs={{0,8},{8,16},{16,24},{24,0},{1,9},{9,17},{17,25},{25,1},{2,10},{10... | collective-permute-start | bytes 3145736 | tf_op jit(solution)/shard_map/ppermute | solution.py:48
  26.1 244.1 %reduce-scatter.2.cloned.1.call-start = ((), (), s32[]{:S(2)}) async-start(), calls=%async_computation.4 | async-start | bytes 5242880 | tf_op jit(solution)/shard_map/reduce_scatter | solution.py:131
  40.3 14.3 %collective-permute-start.3 = (bf16[128,4096]{1,0:T(8,128)(2,1)S(1)}, bf16[128,4096]{1,0:T(8,128)(2,1)}, u32[]{:S(2)}, u32[]{:S(2)}) collective-permute-start(bf16[128,4096]{1,0:T(8,128)(2,1)S(1)} %collective-permute-done.2), channel_id=1, source_target_pairs={{0,8},{8,16},{16,24},{24,0},{1,9},{9,17},{17,25},{25,1},{2,10},{10... | collective-permute-start | bytes 3145736 | tf_op jit(solution)/shard_map/ppermute | solution.py:48
  70.2 70.5 %copy-start.1 = (f32[512,256]{0,1:T(8,128)}, f32[512,256]{0,1:T(8,128)S(1)}, u32[]{:S(2)}) copy-start(f32[512,256]{0,1:T(8,128)S(1)} %fusion.24) | copy-start | bytes 1572868
  143.1 2.3 copy-start.2
  145.4 1.6 copy-start.3
  147.2 8.1 %collective-permute-start = (bf16[512,2,1,128]{3,0,2,1:T(8,128)(2,1)S(1)}, bf16[512,2,1,128]{3,0,2,1:T(8,128)(2,1)S(1)}, u32[]{:S(2)}, u32[]{:S(2)}) collective-permute-start(bf16[512,2,1,128]{3,0,2,1:T(8,128)(2,1)S(1)} %get-tuple-element.431), channel_id=1, source_target_pairs={{0,1},{1,2},{2,3},{3,4},{4,5},{5,6},{6,7},{8,9},{9,10},{10,11},{11... | collective-permute-start | bytes 786440 | tf_op jit(solution)/shard_map/while/body/eval_jaxpr/ppermute | solution.py:15
  159.3 13.6 %collective-permute-start = (bf16[512,2,1,128]{3,0,2,1:T(8,128)(2,1)S(1)}, bf16[512,2,1,128]{3,0,2,1:T(8,128)(2,1)S(1)}, u32[]{:S(2)}, u32[]{:S(2)}) collective-permute-start(bf16[512,2,1,128]{3,0,2,1:T(8,128)(2,1)S(1)} %get-tuple-element.431), channel_id=1, source_target_pairs={{0,1},{1,2},{2,3},{3,4},{4,5},{5,6},{6,7},{8,9},{9,10},{10,11},{11... | collective-permute-start | bytes 786440 | tf_op jit(solution)/shard_map/while/body/eval_jaxpr/ppermute | solution.py:15
Sparse Core Ops, SparseCore 0:
  9.5 51.7 all-gather.3
  63.4 71.3 all-gather.5
  136.9 82.4 all-gather.7
  226.0 44.1 reduce-scatter.1
